TPU v7x, 32 devices: a whole 2x2x4 slice. The times are simulated.
32 devices in a mesh: gx: 16 (over z, y, x), yz: 2 (over core).
Axes of the slice: x: 2, y: 2, z: 4, core: 2. Of those that a mesh axis runs over, the one named last changes fastest.
Arguments:
- magnet: bfloat16 [256, 3, 16, 256], P('yz', None, 'gx'), may hold values from -5 to 5
- newell: bfloat16 [256, 6, 16, 256], P('yz'), may hold values from -0.875 to 0.875
Outputs:
- field: bfloat16 [256, 3, 16, 256], P('yz', None, 'gx')
All inputs are finite; a program needn't handle non-finite values.
Results may differ from a plain program's by a relative error of at most 0.0055.
Values may be sent and summed in bfloat16 or wider, within the bound.
A program may use at most 256 MiB of HBM per device.

v0:
```python
import math

import jax
import jax.numpy as jnp
from jax import lax
from jax.sharding import PartitionSpec as P

EXCHANGE = 0.2


def extended(block, sides, width):
    for axis, dim in sides:
        count = lax.axis_size(axis)
        forward = [(i, i + 1) for i in range(count - 1)]
        forward.append((count - 1, 0))
        backward = [(target, source) for source, target in forward]
        low = lax.ppermute(
            lax.slice_in_dim(block, block.shape[dim] - width, None, axis=dim), axis, forward
        )
        high = lax.ppermute(lax.slice_in_dim(block, 0, width, axis=dim), axis, backward)
        block = jnp.concatenate([low, block, high], axis=dim)
    return block


def dft_tables(row_count, col_count, length, col_first):
    row_ids = jnp.arange(row_count, dtype=jnp.int32)[:, None]
    col_ids = (col_first + jnp.arange(col_count, dtype=jnp.int32))[None, :]
    angles = (row_ids * col_ids % length).astype(jnp.float32) * (2.0 * math.pi / length)
    return (jnp.cos(angles).astype(jnp.bfloat16), jnp.sin(angles).astype(jnp.bfloat16))


def forward_y(z_rows, cos_y, sin_y):
    half_cols = z_rows.shape[-1] // 2
    cos_part = jnp.einsum("ky,ycxq->kcxq", cos_y, z_rows, preferred_element_type=jnp.float32)
    sin_part = jnp.einsum("ky,ycxq->kcxq", sin_y, z_rows, preferred_element_type=jnp.float32)
    return jnp.concatenate(
        [
            cos_part[..., :half_cols] + sin_part[..., half_cols:],
            cos_part[..., half_cols:] - sin_part[..., :half_cols],
        ],
        axis=-1,
    )


def inverse_y(modes_in, cos_y, sin_y):
    half_cols = modes_in.shape[-1] // 2
    cos_part = jnp.einsum("yk,kcxq->ycxq", cos_y, modes_in, preferred_element_type=jnp.float32)
    sin_part = jnp.einsum("yk,kcxq->ycxq", sin_y, modes_in, preferred_element_type=jnp.float32)
    return jnp.concatenate(
        [
            cos_part[..., :half_cols] - sin_part[..., half_cols:],
            cos_part[..., half_cols:] + sin_part[..., :half_cols],
        ],
        axis=-1,
    )


def convolve(kernel_rows, source, tgt_rows):
    src_rows = source.shape[2]
    half_cols = source.shape[3] // 2
    modes = source.shape[0]
    offset = (
        jnp.arange(tgt_rows, dtype=jnp.int32)[:, None]
        - jnp.arange(src_rows, dtype=jnp.int32)[None, :]
    )
    distance = jnp.abs(offset)
    sign_flip = jnp.where(offset >= 0, 1.0, -1.0).astype(jnp.float32)[None, :, :, None]
    picked = jnp.take(kernel_rows, distance.reshape(-1), axis=2).reshape(
        modes, 6, tgt_rows, src_rows, half_cols
    )

    def mix_term(kern_comp, source_comp, imag_part, signed):
        weight = picked[:, kern_comp].astype(jnp.float32)
        if signed:
            weight = weight * sign_flip
        if imag_part:
            values = source[:, source_comp, :, half_cols:]
        else:
            values = source[:, source_comp, :, :half_cols]
        return jnp.sum(weight * values.astype(jnp.float32)[:, None], axis=2)

    x_real = -(
        mix_term(0, 0, False, False) - mix_term(4, 1, True, True) - mix_term(5, 2, True, True)
    )
    x_imag = -(
        mix_term(0, 0, True, False) + mix_term(4, 1, False, True) + mix_term(5, 2, False, True)
    )
    y_real = -(
        -mix_term(4, 0, True, True) + mix_term(1, 1, False, False) + mix_term(3, 2, False, False)
    )
    y_imag = -(
        mix_term(4, 0, False, True) + mix_term(1, 1, True, False) + mix_term(3, 2, True, False)
    )
    z_real = -(
        -mix_term(5, 0, True, True) + mix_term(3, 1, False, False) + mix_term(2, 2, False, False)
    )
    z_imag = -(
        mix_term(5, 0, False, True) + mix_term(3, 1, True, False) + mix_term(2, 2, True, False)
    )
    return jnp.stack(
        [
            jnp.concatenate([x_real, x_imag], axis=-1),
            jnp.concatenate([y_real, y_imag], axis=-1),
            jnp.concatenate([z_real, z_imag], axis=-1),
        ],
        axis=1,
    )


def on_device(magnet, newell):
    y_rows = magnet.shape[0]
    x_cells = magnet.shape[2]
    z_cells = magnet.shape[3]
    ky_rows = newell.shape[0]
    x_total = newell.shape[2]
    y_total = y_rows * lax.axis_size("yz")
    y_first = lax.axis_index("yz") * y_rows
    ky_first = lax.axis_index("yz") * ky_rows
    x_first = lax.axis_index("gx") * x_cells
    cos_z, sin_z = dft_tables(z_cells, z_cells, z_cells, 0)
    z_rows = jnp.dot(
        magnet, jnp.concatenate([cos_z, -sin_z], axis=1), preferred_element_type=jnp.float32
    ).astype(jnp.bfloat16)
    cos_y, sin_y = dft_tables(lax.axis_size("yz") * ky_rows, y_rows, y_total, y_first)
    spectrum = lax.psum_scatter(
        forward_y(z_rows, cos_y, sin_y), "yz", scatter_dimension=0, tiled=True
    ).astype(jnp.bfloat16)
    columns = lax.all_to_all(spectrum, "gx", split_axis=0, concat_axis=2, tiled=True)
    own_rows = columns.shape[0]
    kernel_rows = lax.dynamic_slice_in_dim(newell, lax.axis_index("gx") * own_rows, own_rows, 0)
    conv_out = convolve(kernel_rows, columns, x_total).astype(jnp.bfloat16)
    field_spec = lax.all_to_all(conv_out, "gx", split_axis=2, concat_axis=0, tiled=True)
    cos_y, sin_y = dft_tables(lax.axis_size("yz") * y_rows, ky_rows, y_total, ky_first)
    g_rows = lax.psum_scatter(
        inverse_y(field_spec, cos_y, sin_y), "yz", scatter_dimension=0, tiled=True
    ).astype(jnp.bfloat16)
    demag_field = jnp.dot(
        g_rows, jnp.concatenate([cos_z, -sin_z], axis=0), preferred_element_type=jnp.float32
    ) / (y_total * z_cells)
    padded = extended(magnet, (("gx", 2), ("yz", 0)), 1)
    centre = magnet.astype(jnp.float32)
    beside_all = padded.astype(jnp.float32)
    glob_x = x_first + jnp.arange(x_cells, dtype=jnp.int32)
    has_left = (glob_x > 0).astype(jnp.float32)[None, None, :, None]
    has_right = (glob_x < x_total - 1).astype(jnp.float32)[None, None, :, None]
    laplace = has_right * (beside_all[1:-1, :, 2:] - centre) + has_left * (
        beside_all[1:-1, :, :-2] - centre
    )
    laplace = laplace + beside_all[2:, :, 1:-1] + beside_all[:-2, :, 1:-1] - 2.0 * centre
    laplace = laplace + jnp.roll(centre, 1, 3) + jnp.roll(centre, -1, 3) - 2.0 * centre
    return (demag_field + EXCHANGE * laplace).astype(jnp.bfloat16)


def solution(mesh):
    return jax.shard_map(
        on_device,
        mesh=mesh,
        in_specs=(P("yz", None, "gx", None), P("yz", None, None, None)),
        out_specs=P("yz", None, "gx", None),
        check_vma=False,
    )
```

profile of v0, /device:TPU:0, one launch (start us, length us, event | category | flops | bytes accessed | tf_op | source)
XLA Modules:
  0.0 97.2 jit_solution(9016384387048133065)
XLA Ops:
  6.5 0.0 reduce-scatter.3.cloned.1.call-start
  6.5 1.0 %cosine_convert_fusion = bf16[256,256]{0,1:T(8,128)(2,1)S(1)} fusion(), kind=kLoop, calls=%fused_computation.96 | loop fusion | flops 983040 | bytes 131072 | tf_op jit(solution)/shard_map/convert_element_type | solution.py:29
  7.5 1.0 %fusion.59 = bf16[256,256]{0,1:T(8,128)(2,1)S(1)} fusion(), kind=kLoop, calls=%fused_computation.107 | loop fusion | flops 1179648 | bytes 131072 | tf_op jit(solution)/shard_map/neg | solution.py:122
  8.5 1.2 %fusion.26 = bf16[128,3,512]{0,2,1:T(8,128)(2,1)S(1)} fusion(bf16[256,256]{0,1:T(8,128)(2,1)S(1)} %fusion.59, bf16[256,256]{0,1:T(8,128)(2,1)S(1)} %cosine_convert_fusion, bf16[128,3,1,256]{3,0,2,1:T(8,128)(2,1)} %param.2), kind=kOutput, calls=%fused_computation.47 | convolution fusion | flops 101384192 | bytes 851968 | tf_op jit(solution)/shard_map/dot_general | solution.py:121
  9.8 0.8 convolution_bitcast_fusion.2
  10.6 0.8 convolution_bitcast_fusion.3
  11.3 0.2 slice_add_fusion.1
  11.5 1.3 %pad_maximum_fusion = f32[256,3,1,512]{3,0,1,2:T(8,128)} fusion(f32[256,3,1,256]{3,0,1,2:T(8,128)S(1)} %get-tuple-element.50, f32[256,3,1,256]{3,0,1,2:T(8,128)S(1)} %get-tuple-element.49), kind=kLoop, calls=%fused_computation.40 | loop fusion | flops 393216 | bytes 3145728 | tf_op jit(solution)/shard_map/concatenate | solution.py:36
  12.9 0.0 reduce-scatter.3.cloned.1.call-update
  12.9 1.0 %constant_dynamic-slice_fusion = bf16[8,6,16,256]{3,2,1,0:T(8,128)(2,1)S(1)} fusion(bf16[128,6,16,256]{3,2,1,0:T(8,128)(2,1)} %param.3, s32[]{:T(128)S(6)} %select_n.58), kind=kLoop, calls=%fused_computation.151 | loop fusion | bytes 786436 | tf_op jit(solution)/shard_map/dynamic_slice | solution.py:130
  13.9 0.2 copy.62
  14.2 0.1 abs.20
  14.3 4.0 %gather_fusion = bf16[256,8,6,256]{3,1,2,0:T(8,128)(2,1)} fusion(bf16[8,6,16,256]{3,0,2,1:T(8,128)(2,1)S(1)} %copy.62, s32[1024]{0:T(1024)S(1)} %pad_clamp_fusion), kind=kCustom, calls=%fused_computation | custom fusion | bytes 12583936 | tf_op jit(solution)/shard_map/jit(_take)/gather | solution.py:68
  18.3 6.5 %reduce-scatter.3.cloned.1.call-done = f32[128,3,1,512]{3,0,1,2:T(8,128)} async-done(((f32[256,3,1,512]{3,0,1,2:T(8,128)}), f32[128,3,1,512]{3,0,1,2:T(8,128)}) %reduce-scatter.3.cloned.1.call-update) | async-done | bytes 786448 | tf_op jit(solution)/shard_map/reduce_scatter | solution.py:125
  24.7 1.2 %convert_element_type.144 = bf16[128,3,1,512]{3,0,1,2:T(8,128)(2,1)S(1)} convert(f32[128,3,1,512]{3,0,1,2:T(8,128)} %reduce-scatter.3.cloned.1.call-done) | non-fusion elementwise | flops 196608 | bytes 1179648 | tf_op jit(solution)/shard_map/convert_element_type | solution.py:127
  25.9 1.2 %copy.40 = bf16[128,3,1,512]{3,1,2,0:T(4,128)(2,1)} copy(bf16[128,3,1,512]{3,0,1,2:T(8,128)(2,1)S(1)} %convert_element_type.144) | data formatting | bytes 786432 | tf_op jit(solution)/shard_map/convert_element_type | solution.py:127
  27.1 6.9 %all-to-all-start = ((bf16[128,3,1,512]{3,1,2,0:T(4,128)(2,1)}), bf16[128,3,1,512]{3,1,2,0:T(4,128)(2,1)S(1)}, u32[]{:S(2)}, u32[]{:S(2)}) async-start(bf16[128,3,1,512]{3,1,2,0:T(4,128)(2,1)} %copy.40), calls=%async_computation.1 | async-start | bytes 1048576 | tf_op jit(solution)/shard_map/all_to_all | solution.py:128
  34.0 0.0 reduce-scatter.5.cloned.1.call-start
  34.1 6.1 %broadcast_select_fusion = bf16[8,6,16,16,256]{4,0,1,3,2:T(8,128)(2,1)} fusion(bf16[8,6,16,16,256]{4,0,1,3,2:T(8,128)(2,1)} %bitcast.153, pred[16,16]{1,0:T(8,128)(4,1)S(1)} %compare_and_fusion), kind=kLoop, calls=%fused_computation.1 | loop fusion | flops 3145728 | bytes 12583168 | tf_op jit(solution)/shard_map/jit(_take)/select_n | solution.py:68
  40.2 9.2 %all-to-all-done = bf16[128,3,1,512]{3,1,2,0:T(4,128)(2,1)S(1)} async-done(((bf16[128,3,1,512]{3,1,2,0:T(4,128)(2,1)}), bf16[128,3,1,512]{3,1,2,0:T(4,128)(2,1)S(1)}, u32[]{:S(2)}, u32[]{:S(2)}) %all-to-all-start) | async-done | bytes 393248 | tf_op jit(solution)/shard_map/all_to_all | solution.py:128
  49.4 0.6 slice_convert_fusion.1
  50.1 7.9 %fusion.25 = (f32[8,16,256]{2,0,1:T(8,128)S(1)}, f32[8,16,256]{2,0,1:T(8,128)S(1)}, f32[8,16,256]{2,0,1:T(8,128)S(1)}, f32[8,16,256]{2,0,1:T(8,128)S(1)}, f32[8,...) fusion(f32[16,16]{1,0:T(8,128)S(1)} %fusion.71, ...), kind=kLoop, calls=%fused_computation.39 | loop fusion | flops 22478848 | bytes 9438208 | tf_op jit(solution)/shard_map/reduce_sum | solution.py:80
  58.4 15.6 %all_to_all.33 = bf16[8,3,16,512]{3,0,1,2:T(8,128)(2,1)S(1)} all-to-all(bf16[8,3,16,512]{3,0,1,2:T(8,128)(2,1)S(1)} %pad_maximum_fusion.2), channel_id=1, replica_groups=mesh['gx'=16,'yz'=2] {'gx'}, dimensions={2} | all-to-all | bytes 786432 | tf_op jit(solution)/shard_map/all_to_all | solution.py:132
  74.0 0.8 convolution_bitcast_fusion.1
  74.7 0.8 convolution_bitcast_fusion
  75.5 0.2 slice_subtract_fusion
  75.7 0.0 copy-start
  75.7 1.4 %pad_maximum_fusion.1 = f32[256,3,1,512]{3,0,1,2:T(8,128)} fusion(f32[256,3,1,256]{3,0,1,2:T(8,128)S(1)} %get-tuple-element.48, f32[256,3,1,256]{3,0,1,2:T(8,128)S(1)} %get-tuple-element.47), kind=kLoop, calls=%fused_computation.41 | loop fusion | flops 393216 | bytes 3145728 | tf_op jit(solution)/shard_map/concatenate | solution.py:49
  77.1 0.0 reduce-scatter.5.cloned.1.call-update
  77.1 0.0 copy-done
  77.1 0.6 collective-permute-start
  77.7 5.1 %collective-permute-start.1 = (bf16[128,3,1,256]{3,0,1,2:T(8,128)(2,1)S(1)}, bf16[128,3,1,256]{3,0,1,2:T(8,128)(2,1)S(1)}, u32[]{:S(2)}, u32[]{:S(2)}) collective-permute-start(bf16[128,3,1,256]{3,0,1,2:T(8,128)(2,1)S(1)} %bitcast.156), channel_id=1, source_target_pairs={{2,0},{4,2},{6,4},{8,6},{10,8},{12,10},{14,12},{16,14},{18,16},{20... | collective-permute-start | bytes 589832 | tf_op jit(solution)/shard_map/ppermute | solution.py:20
  82.8 0.2 fusion.90
  83.0 3.5 %collective-permute-done = bf16[128,3,1,256]{3,0,1,2:T(8,128)(2,1)S(1)} collective-permute-done((bf16[128,3,1,256]{3,0,1,2:T(8,128)(2,1)S(1)}, bf16[128,3,1,256]{3,0,1,2:T(8,128)(2,1)S(1)}, u32[]{:S(2)}, u32[]{:S(2)}) %collective-permute-start) | collective-permute-done | bytes 196640 | tf_op jit(solution)/shard_map/ppermute | solution.py:17
  86.5 0.0 collective-permute-done.1
  86.5 0.1 collective-permute-start.2
  86.6 0.5 collective-permute-start.3
  87.1 0.1 fusion.91
  87.2 0.5 collective-permute-done.2
  87.8 0.2 collective-permute-done.3
  88.0 0.1 maximum_convert_fusion
  88.1 0.0 reduce-scatter.5.cloned.1.call-done
  88.1 2.3 %fusion.30 = bf16[128,3,1,256]{3,0,2,1:T(8,128)(2,1)} fusion(f32[130,3,3,256]{3,0,1,2:T(8,128)S(1)} %maximum_convert_fusion, f32[128,3,1,255]{3,0,1,2:T(8,128)S(1)} %get-tuple-element.60, f32[128,3,1,1]{3,0,1,2:T(8,128)S(1)} %get-tuple-element.62, f32[128,3,1,1]{3,0,1,2:T(8,128)S(1)} %get-tuple-element.61, f32[128,3,1,255]{3,0,1,2:T(8,128)S(1)} %get-tuple-element.59, ...), kind=kOutput, calls=%fused_computation.52 | convolution fusion | flops 103251968 | bytes 3801096 | tf_op jit(solution)/shard_map/dot_general | solution.py:137
  (21 shorter events, 0.4 us)
Async XLA Ops:
  6.5 18.2 %reduce-scatter.3.cloned.1.call-start = ((), (), s32[]{:S(2)}) async-start(), calls=%async_computation.4 | async-start | bytes 2359296 | tf_op jit(solution)/shard_map/reduce_scatter | solution.py:125
  27.1 22.3 %all-to-all-start = ((bf16[128,3,1,512]{3,1,2,0:T(4,128)(2,1)}), bf16[128,3,1,512]{3,1,2,0:T(4,128)(2,1)S(1)}, u32[]{:S(2)}, u32[]{:S(2)}) async-start(bf16[128,3,1,512]{3,1,2,0:T(4,128)(2,1)} %copy.40), calls=%async_computation.1 | async-start | bytes 1048576 | tf_op jit(solution)/shard_map/all_to_all | solution.py:128
  34.0 54.1 %reduce-scatter.5.cloned.1.call-start = ((), (), s32[]{:S(2)}) async-start(), calls=%async_computation.5 | async-start | bytes 2359296 | tf_op jit(solution)/shard_map/reduce_scatter | solution.py:134
  75.7 1.4 %copy-start = (bf16[128,3,1,256]{3,0,2,1:T(8,128)(2,1)S(1)}, bf16[128,3,1,256]{3,0,2,1:T(8,128)(2,1)}, u32[]{:S(2)}) copy-start(bf16[128,3,1,256]{3,0,2,1:T(8,128)(2,1)} %param.2) | copy-start | bytes 589828
  77.1 9.4 %collective-permute-start = (bf16[128,3,1,256]{3,0,1,2:T(8,128)(2,1)S(1)}, bf16[128,3,1,256]{3,0,1,2:T(8,128)(2,1)S(1)}, u32[]{:S(2)}, u32[]{:S(2)}) collective-permute-start(bf16[128,3,1,256]{3,0,1,2:T(8,128)(2,1)S(1)} %bitcast.155), channel_id=1, source_target_pairs={{0,2},{2,4},{4,6},{6,8},{8,10},{10,12},{12,14},{14,16},{16,18},{18... | collective-permute-start | bytes 589832 | tf_op jit(solution)/shard_map/ppermute | solution.py:17
  77.7 8.8 %collective-permute-start.1 = (bf16[128,3,1,256]{3,0,1,2:T(8,128)(2,1)S(1)}, bf16[128,3,1,256]{3,0,1,2:T(8,128)(2,1)S(1)}, u32[]{:S(2)}, u32[]{:S(2)}) collective-permute-start(bf16[128,3,1,256]{3,0,1,2:T(8,128)(2,1)S(1)} %bitcast.156), channel_id=1, source_target_pairs={{2,0},{4,2},{6,4},{8,6},{10,8},{12,10},{14,12},{16,14},{18,16},{20... | collective-permute-start | bytes 589832 | tf_op jit(solution)/shard_map/ppermute | solution.py:20
  86.5 1.2 %collective-permute-start.2 = (bf16[1,3,3,256]{3,0,1,2:T(2,128)(2,1)S(1)}, bf16[1,3,3,256]{3,0,1,2:T(2,128)(2,1)S(1)}, u32[]{:S(2)}, u32[]{:S(2)}) collective-permute-start(bf16[1,3,3,256]{3,0,1,2:T(2,128)(2,1)S(1)} %get-tuple-element.51), channel_id=1, source_target_pairs={{0,1},{1,0},{2,3},{3,2},{4,5},{5,4},{6,7},{7,6},{8,9},{9,8},{10,11... | collective-permute-start | bytes 13832 | tf_op jit(solution)/shard_map/ppermute | solution.py:17
  86.6 1.3 %collective-permute-start.3 = (bf16[1,3,3,256]{3,0,1,2:T(2,128)(2,1)S(1)}, bf16[1,3,3,256]{3,0,1,2:T(2,128)(2,1)S(1)}, u32[]{:S(2)}, u32[]{:S(2)}) collective-permute-start(bf16[1,3,3,256]{3,0,1,2:T(2,128)(2,1)S(1)} %get-tuple-element.52), channel_id=1, source_target_pairs={{1,0},{0,1},{3,2},{2,3},{5,4},{4,5},{7,6},{6,7},{9,8},{8,9},{11,10... | collective-permute-start | bytes 13832 | tf_op jit(solution)/shard_map/ppermute | solution.py:20
Sparse Core Ops, SparseCore 0:
  13.0 11.6 reduce-scatter.2
  77.2 6.9 reduce-scatter.4
where the time goes:
time: 97.7 us; the launch traced here: 97.2 us
  other arithmetic  21.3 us (22%)
  waiting for transfers between devices  20 us (20%)
  blocking collectives  15.6 us (16%)
  between operations  13.7 us (14%)
  starting transfers between devices  13.2 us (14%)
  local copies, waits for them, and re-layouts  6.86 us (7%)
  matrix products  6.61 us (7%)
    all_to_all x1, blocking collectives, on_device(): lax.all_to_all(conv_out, 'gx', split_axis=2, concat_axis=0, tiled=True)  15.6 us
    all_to_all x1, waiting for transfers between devices, on_device(): lax.all_to_all(spectrum, 'gx', split_axis=0, concat_axis=2, tiled=True)  9.24 us
    reduce_sum x1, other arithmetic, mix_term(): return jnp.sum(weight * values.astype(jnp.float32)[:, None], axis=2)  7.94 us
    all_to_all x1, starting transfers between devices, on_device(): lax.all_to_all(spectrum, 'gx', split_axis=0, concat_axis=2, tiled=True)  6.89 us
    reduce_scatter x1, waiting for transfers between devices, on_device(): lax.psum_scatter(forward_y(z_rows, cos_y, sin_y), 'yz', scatter_dimension...  6.46 us
    select_n x2, other arithmetic, convolve(): jnp.take(kernel_rows, distance.reshape(-1), axis=2)  6.1 us
    ppermute x2, starting transfers between devices, extended(): lax.ppermute(lax.slice_in_dim(block, 0, width, axis=dim), axis, backward)  5.56 us
    ppermute x2, waiting for transfers between devices, extended(): lax.ppermute(lax.slice_in_dim(block, block.shape[dim] - width, None, axis...  4.05 us
  transfers between devices with their start and end apart: 7, of which 5 were waited for; matrix products, arithmetic and copies ran while one was open for 12% of the time, Pallas kernels for 0%

commit v1 on v0

v1 whole, which is shorter than its diff:
```python
import functools
import math

import jax
import jax.numpy as jnp
import ml_dtypes
import numpy as np
from jax import lax
from jax.experimental import pallas as pl
from jax.experimental.pallas import tpu as pltpu
from jax.sharding import PartitionSpec as P

EXCHANGE = 0.2
F32 = jnp.float32
BF16 = jnp.bfloat16
MESH = pl.DeviceIdType.MESH


def ky_owned(groups, parts, pairs, length):
    order = []
    for part in range(parts):
        for g in range(groups):
            first = [(g * parts + part) * pairs + p for p in range(pairs)]
            mirror = [(length - t) if t else length // 2 for t in first]
            order.append(first + mirror)
    return np.array(order).reshape(parts, -1)


def tables(groups, parts, y_total, z_total):
    pairs = y_total // (groups * parts * 2)
    rows = y_total // parts
    order = ky_owned(groups, parts, pairs, y_total)

    def trig(k, n, length):
        angle = (k[:, None] * n[None, :] % length) * (2.0 * math.pi / length)
        return np.cos(angle), np.sin(angle)

    forward, inverse = [], []
    for part in range(parts):
        own_first = (np.arange(y_total) + part * rows) % y_total
        forward.append(np.stack(trig(order[part], own_first, y_total)))
        inverse.append(np.stack(trig(own_first[:rows], order.reshape(-1), y_total)))
    half = z_total // 2
    cos, sin = trig(np.arange(z_total), np.arange(half), z_total)
    alternate = np.cos(math.pi * np.arange(z_total))
    z_fwd = np.concatenate([cos, -sin], axis=1)
    z_fwd[:, half] = alternate
    z_inv = -np.concatenate([cos, -sin], axis=1).T
    z_inv[0] = -0.5
    z_inv[half] = -0.5 * alternate
    reverse = np.zeros((z_total, half))
    for k in range(half):
        reverse[-k % z_total, k] = 1.0
    cast = lambda a: np.asarray(a, np.float32).astype(ml_dtypes.bfloat16)
    return (
        cast(np.stack(forward)),
        cast(np.stack(inverse)),
        cast(z_fwd),
        cast(z_inv),
        cast(reverse),
    )


def kernel(
    groups, pairs, magnet, newell, y_fwd, y_inv, z_fwd, z_inv, rev, out,
    mag, nwl, yf, yi, zf, zi, rv, halo, spec, send, recv, kern, source, back, fields, stack,
    lap, result, load_sem, nwl_sem, pair_sem, halo_sem, fwd_send, fwd_recv, bwd_send, bwd_recv,
    rel_send, rel_recv, out_sem,
):
    g = lax.axis_index("gx")
    c = lax.axis_index("yz")
    other = 1 - c
    own = 2 * pairs
    rows = magnet.shape[1]
    cells = groups
    half = magnet.shape[2] // 2

    barrier = pltpu.get_barrier_semaphore()
    for r in range(1, groups):
        pl.semaphore_signal(
            barrier, inc=1, device_id=(lax.rem(g + r, groups), c), device_id_type=MESH
        )
    pl.semaphore_signal(barrier, inc=1, device_id=(g, other), device_id_type=MESH)

    loads = []
    for comp in range(3):
        loads.append(
            pltpu.make_async_copy(
                magnet.at[comp], mag.at[comp, pl.ds(0, rows), :], load_sem.at[comp]
            )
        )
    loads.append(pltpu.make_async_copy(z_fwd, zf, load_sem.at[3]))
    loads.append(pltpu.make_async_copy(y_fwd.at[c], yf, load_sem.at[4]))
    loads.append(pltpu.make_async_copy(rev, rv, load_sem.at[5]))
    loads.append(pltpu.make_async_copy(y_inv.at[c], yi, load_sem.at[6]))
    loads.append(pltpu.make_async_copy(z_inv, zi, load_sem.at[7]))
    for copy in loads:
        copy.start()

    def newell_row(part, p):
        t = (2 * g + part) * pairs + p
        return (1 - c) * t + c * lax.rem(rows - t, rows)

    near = [
        pltpu.make_async_copy(newell.at[newell_row(c, p)], nwl.at[c, p], nwl_sem.at[p])
        for p in range(pairs)
    ]
    for copy in near:
        copy.start()

    pl.semaphore_wait(barrier, groups)

    for comp in range(3):
        loads[comp].wait()
    swap = []
    for comp in range(3):
        swap.append(
            pltpu.make_async_remote_copy(
                src_ref=mag.at[comp, pl.ds(0, rows), :],
                dst_ref=mag.at[comp, pl.ds(rows, rows), :],
                send_sem=pair_sem.at[0, comp],
                recv_sem=pair_sem.at[1, comp],
                device_id=(g, other),
                device_id_type=MESH,
            )
        )
    for copy in swap:
        copy.start()
    far = []
    for p in range(pairs):
        far.append(
            pltpu.make_async_remote_copy(
                src_ref=newell.at[newell_row(other, p)],
                dst_ref=nwl.at[c, p],
                send_sem=pair_sem.at[0, 3 + p],
                recv_sem=pair_sem.at[1, 3 + p],
                device_id=(g, other),
                device_id_type=MESH,
            )
        )
    for copy in far:
        copy.start()

    loads[3].wait()
    loads[4].wait()
    for comp in range(3):
        swap[comp].wait_recv()
        z_rows = jnp.dot(mag[comp], zf[...], preferred_element_type=F32).astype(BF16)
        cos_part = jnp.dot(yf[0], z_rows, preferred_element_type=F32)
        sin_part = jnp.dot(yf[1], z_rows, preferred_element_type=F32)
        low = 2 * comp * half
        spec[:, pl.ds(low, half)] = cos_part[:, :half] + sin_part[:, half:]
        spec[:, pl.ds(low + half, half)] = cos_part[:, half:] - sin_part[:, :half]
    for i in range(groups):
        send[i] = spec[pl.ds(i * own, own), :].astype(BF16)

    forward = []
    for r in range(1, groups):
        to = lax.rem(g + r, groups)
        forward.append(
            pltpu.make_async_remote_copy(
                src_ref=send.at[to],
                dst_ref=recv.at[g],
                send_sem=fwd_send.at[r],
                recv_sem=fwd_recv.at[r],
                device_id=(to, c),
                device_id_type=MESH,
            )
        )
    for copy in forward:
        copy.start()
    recv[g] = send[g]

    up = pltpu.make_async_remote_copy(
        src_ref=mag.at[:, pl.ds(0, rows), :],
        dst_ref=halo.at[0],
        send_sem=halo_sem.at[0],
        recv_sem=halo_sem.at[1],
        device_id=(lax.rem(g + 1, groups), c),
        device_id_type=MESH,
    )
    down = pltpu.make_async_remote_copy(
        src_ref=mag.at[:, pl.ds(0, rows), :],
        dst_ref=halo.at[1],
        send_sem=halo_sem.at[2],
        recv_sem=halo_sem.at[3],
        device_id=(lax.rem(g + groups - 1, groups), c),
        device_id_type=MESH,
    )

    @pl.when(g < groups - 1)
    def _():
        up.start()

    @pl.when(g > 0)
    def _():
        down.start()

    for copy in near:
        copy.wait()
    for copy in far:
        copy.wait_recv()
    loads[5].wait()
    table_rows = 6 * cells
    even_rows = 4 * cells
    lane0 = lax.broadcasted_iota(jnp.int32, (table_rows, half), 1) == 0
    even = lax.broadcasted_iota(jnp.int32, (table_rows, half), 0) < even_rows
    sign = jnp.where(even, 1.0, -1.0).astype(F32)
    for p in range(pairs):
        first = nwl[0, p].reshape(table_rows, 2 * half)
        mirror = nwl[1, p].reshape(table_rows, 2 * half)
        rev_first = jnp.dot(first, rv[...], preferred_element_type=F32)
        rev_mirror = jnp.dot(mirror, rv[...], preferred_element_type=F32)
        lo_first, hi_first = first[:, :half].astype(F32), first[:, half:].astype(F32)
        lo_mirror, hi_mirror = mirror[:, :half].astype(F32), mirror[:, half:].astype(F32)
        if p == 0:
            alone = ((2 * g + c) * pairs == 0).astype(F32)
            paired = 1.0 - alone
            of_first = alone * rev_first + paired * rev_mirror
            of_mirror = alone * rev_mirror + paired * rev_first
        else:
            of_first, of_mirror = rev_mirror, rev_first
        k_first = lo_first + sign * of_first
        k_mirror = lo_mirror + sign * of_mirror
        middle = hi_first + sign * hi_mirror
        if p == 0:
            i_first = jnp.where(lane0, alone * (2.0 * hi_first) + paired * k_first, k_first)
            i_mirror = jnp.where(lane0, alone * (2.0 * hi_mirror) + paired * middle, k_mirror)
            k_mirror = jnp.where(lane0, alone * k_mirror + paired * middle, k_mirror)
        else:
            k_mirror = jnp.where(lane0, middle, k_mirror)
            i_first, i_mirror = k_first, k_mirror
        kern[pl.ds(p, table_rows, stride=own), :] = k_first
        kern[pl.ds(pairs + p, table_rows, stride=own), :] = k_mirror
        base = table_rows * own
        kern[pl.ds(base + p, even_rows, stride=own), :] = i_first[:even_rows]
        kern[pl.ds(base + pairs + p, even_rows, stride=own), :] = i_mirror[:even_rows]

    for comp in range(3):
        full = mag[comp].astype(F32)
        centre = full[:rows]
        total = pltpu.roll(full, 1, 0)[:rows] + pltpu.roll(full, 2 * rows - 1, 0)[:rows]
        total = total + pltpu.roll(centre, 1, 1) + pltpu.roll(centre, 2 * half - 1, 1)
        lap[comp] = total - 4.0 * centre

    lane = lax.broadcasted_iota(jnp.int32, (own, half), 1)
    slot = lax.broadcasted_iota(jnp.int32, (own, half), 0)
    first_t = (2 * g + c) * pairs + lax.rem(slot, pairs)
    packed = jnp.logical_and(lane == 0, first_t > 0)
    at_first = jnp.logical_and(packed, slot < pairs)
    at_mirror = jnp.logical_and(packed, slot >= pairs)

    def flip(v):
        return jnp.concatenate([v[pairs:], v[:pairs]], axis=0)

    def unpack(j):
        block = recv[j].astype(F32)
        for comp in range(3):
            re = block[:, 2 * comp * half : (2 * comp + 1) * half]
            im = block[:, (2 * comp + 1) * half : (2 * comp + 2) * half]
            re_f, im_f = flip(re), flip(im)
            new_re = jnp.where(at_first, 0.5 * (re + re_f), jnp.where(at_mirror, 0.5 * (im + im_f), re))
            new_im = jnp.where(at_first, 0.5 * (im - im_f), jnp.where(at_mirror, 0.5 * (re - re_f), im))
            source[j, 2 * comp] = new_re
            source[j, 2 * comp + 1] = new_im

    unpack(g)
    for r in range(1, groups):
        forward[r - 1].wait_recv()
        unpack(lax.rem(g + groups - r, groups))

    def k_of(entry, d):
        start = pl.multiple_of((entry * cells + d) * own, own)
        return kern[pl.ds(start, own), :]

    def couple(i, carry):
        acc = [jnp.zeros((own, half), F32) for _ in range(6)]
        for j in range(cells):
            d = jnp.abs(i - j)
            s = jnp.where(i >= j, 1.0, -1.0).astype(F32)
            xx, yy, zz, yz = (k_of(e, d) for e in range(4))
            xy, xz = s * k_of(4, d), s * k_of(5, d)
            xxi, yyi, zzi, yzi = (k_of(6 + e, d) for e in range(4))
            xr, xi, yr, yim, zr, zim = (source[j, q] for q in range(6))
            acc[0] += xx * xr - xy * yim - xz * zim
            acc[1] += xxi * xi + xy * yr + xz * zr
            acc[2] += yy * yr + yz * zr - xy * xi
            acc[3] += yyi * yim + yzi * zim + xy * xr
            acc[4] += yz * yr + zz * zr - xz * xi
            acc[5] += yzi * yim + zzi * zim + xz * xr
        for comp in range(3):
            re, im = acc[2 * comp], acc[2 * comp + 1]
            re_f, im_f = flip(re), flip(im)
            new_re = jnp.where(at_first, re - im_f, jnp.where(at_mirror, re_f + im, re))
            new_im = jnp.where(at_first, im + re_f, jnp.where(at_mirror, re - im_f, im))
            back[i, :, pl.ds(2 * comp * half, half)] = new_re.astype(BF16)
            back[i, :, pl.ds((2 * comp + 1) * half, half)] = new_im.astype(BF16)
        return carry

    lax.fori_loop(0, cells, couple, 0)

    backward = []
    for r in range(1, groups):
        to = lax.rem(g + r, groups)
        backward.append(
            pltpu.make_async_remote_copy(
                src_ref=back.at[to],
                dst_ref=fields.at[c, g],
                send_sem=bwd_send.at[r],
                recv_sem=bwd_recv.at[r],
                device_id=(to, c),
                device_id_type=MESH,
            )
        )
    for copy in backward:
        copy.start()
    fields[c, g] = back[g]

    def relay(r):
        who = lax.rem(g + groups - r, groups)
        return pltpu.make_async_remote_copy(
            src_ref=fields.at[c, who],
            dst_ref=fields.at[c, who],
            send_sem=rel_send.at[r],
            recv_sem=rel_recv.at[r],
            device_id=(g, other),
            device_id_type=MESH,
        )

    relays = [relay(r) for r in range(groups)]
    relays[0].start()

    @pl.when(g == 0)
    def _():
        halo[0] = mag[:, pl.ds(0, rows), :]

    @pl.when(g > 0)
    def _():
        up.wait_recv()

    @pl.when(g == groups - 1)
    def _():
        halo[1] = mag[:, pl.ds(0, rows), :]

    @pl.when(g < groups - 1)
    def _():
        down.wait_recv()

    for comp in range(3):
        centre = mag[comp, pl.ds(0, rows), :].astype(F32)
        x_part = halo[0, comp].astype(F32) + halo[1, comp].astype(F32) - 2.0 * centre
        lap[comp] = EXCHANGE * (lap[comp] + x_part)

    for r in range(1, groups):
        backward[r - 1].wait_recv()
        relays[r].start()
    for r in range(groups):
        relays[r].wait_recv()
    for part in range(2):
        for i in range(groups):
            stack[pl.ds((part * groups + i) * own, own), :] = fields[part, i].astype(F32)

    loads[6].wait()
    loads[7].wait()
    scale = 1.0 / (2 * rows * 2 * half)
    writes = []
    for comp in range(3):
        modes = stack[:, pl.ds(2 * comp * half, 2 * half)].astype(BF16)
        cos_part = jnp.dot(yi[0], modes, preferred_element_type=F32)
        sin_part = jnp.dot(yi[1], modes, preferred_element_type=F32)
        g_rows = jnp.concatenate(
            [
                cos_part[:, :half] - sin_part[:, half:],
                cos_part[:, half:] + sin_part[:, :half],
            ],
            axis=1,
        ).astype(BF16)
        demag = jnp.dot(g_rows, zi[...], preferred_element_type=F32) * scale
        result[comp] = (demag + lap[comp]).astype(BF16)
        write = pltpu.make_async_copy(result.at[comp], out.at[comp], out_sem.at[comp])
        write.start()
        writes.append(write)

    for copy in swap + far + forward + backward + relays:
        copy.wait_send()

    @pl.when(g < groups - 1)
    def _():
        up.wait_send()

    @pl.when(g > 0)
    def _():
        down.wait_send()

    for write in writes:
        write.wait()


def on_device(magnet, newell, *consts):
    rows, _, x_cells, z_total = magnet.shape
    groups = lax.axis_size("gx")
    parts = lax.axis_size("yz")
    assert x_cells == 1 and parts == 2
    y_total = rows * parts
    pairs = y_total // (groups * parts * 2)
    own = 2 * pairs
    half = z_total // 2
    wide = 3 * z_total
    any_ref = pl.BlockSpec(memory_space=pl.ANY)
    dma = pltpu.SemaphoreType.DMA
    planes = jnp.transpose(magnet[:, :, 0, :], (1, 0, 2))
    field = pl.pallas_call(
        functools.partial(kernel, groups, pairs),
        out_shape=jax.ShapeDtypeStruct(planes.shape, BF16),
        in_specs=[any_ref] * 7,
        out_specs=any_ref,
        scratch_shapes=[
            pltpu.VMEM((3, y_total, z_total), BF16),
            pltpu.VMEM((2, pairs, 6, groups, z_total), BF16),
            pltpu.VMEM((2, rows, y_total), BF16),
            pltpu.VMEM((2, rows, y_total), BF16),
            pltpu.VMEM((z_total, z_total), BF16),
            pltpu.VMEM((z_total, z_total), BF16),
            pltpu.VMEM((z_total, half), BF16),
            pltpu.VMEM((2, 3, rows, z_total), BF16),
            pltpu.VMEM((rows, wide), F32),
            pltpu.VMEM((groups, own, wide), BF16),
            pltpu.VMEM((groups, own, wide), BF16),
            pltpu.VMEM((10 * groups * own, half), F32),
            pltpu.VMEM((groups, 6, own, half), F32),
            pltpu.VMEM((groups, own, wide), BF16),
            pltpu.VMEM((2, groups, own, wide), BF16),
            pltpu.VMEM((y_total, wide), F32),
            pltpu.VMEM((3, rows, z_total), F32),
            pltpu.VMEM((3, rows, z_total), BF16),
            dma((8,)),
            dma((pairs,)),
            dma((2, 3 + pairs)),
            dma((4,)),
            dma((groups,)),
            dma((groups,)),
            dma((groups,)),
            dma((groups,)),
            dma((groups,)),
            dma((groups,)),
            dma((3,)),
        ],
        compiler_params=pltpu.CompilerParams(collective_id=0, has_side_effects=True),
    )(planes, newell, *consts)
    return jnp.transpose(field, (1, 0, 2))[:, :, None, :]


def solution(mesh):
    groups, parts = mesh.shape["gx"], mesh.shape["yz"]

    def run(magnet, newell):
        consts = tables(groups, parts, magnet.shape[0], magnet.shape[3])
        body = lambda m, n: on_device(m, n, *[jnp.asarray(t) for t in consts])
        return jax.shard_map(
            body,
            mesh=mesh,
            in_specs=(P("yz", None, "gx", None), P("yz", None, None, None)),
            out_specs=P("yz", None, "gx", None),
            check_vma=False,
        )(magnet, newell)

    return run
```

time: 97.7 us -> 28.4 us (0.29)
  Pallas kernels: 0 us -> 26.6 us
  other arithmetic: 21.3 us -> 0 us
  waiting for transfers between devices: 20 us -> 0 us
  blocking collectives: 15.6 us -> 0 us
  between operations: 13.7 us -> 0.01 us
  starting transfers between devices: 13.2 us -> 0 us
  matrix products: 6.61 us -> 0 us
  local copies, waits for them, and re-layouts: 6.86 us -> 1.62 us
    pallas_call x0 -> x1, Pallas kernels: none -> 26.6 us  [on_device(): pl.pallas_call(functools.partial(kernel, groups, pairs), out_shape=jax.Sh...]
    all_to_all x1 -> x0, blocking collectives: 15.6 us -> none  [on_device(): lax.all_to_all(conv_out, 'gx', split_axis=2, concat_axis=0, tiled=True)]
    all_to_all x1 -> x0, waiting for transfers between devices: 9.24 us -> none  [on_device(): lax.all_to_all(spectrum, 'gx', split_axis=0, concat_axis=2, tiled=True)]
    reduce_sum x1 -> x0, other arithmetic: 7.94 us -> none  [mix_term(): return jnp.sum(weight * values.astype(jnp.float32)[:, None], axis=2)]
    all_to_all x1 -> x0, starting transfers between devices: 6.89 us -> none  [on_device(): lax.all_to_all(spectrum, 'gx', split_axis=0, concat_axis=2, tiled=True)]
    dot_general x6 -> x0, matrix products: 6.61 us -> none  [the longest x1 2.28 us: on_device(): jnp.dot(g_rows, jnp.concatenate([cos_z, -sin_z], axis=0), preferred_eleme...]
    reduce_scatter x2 -> x0, waiting for transfers between devices: 6.48 us -> none  [the longest x1 6.46 us: on_device(): lax.psum_scatter(forward_y(z_rows, cos_y, sin_y), 'yz', scatter_dimension...]
    ppermute x4 -> x0, starting transfers between devices: 6.24 us -> none  [the longest x2 5.56 us: extended(): lax.ppermute(lax.slice_in_dim(block, 0, width, axis=dim), axis, backward)]
  transfers between devices with their start and end apart: 7 -> 0, of which waited for: 5 -> 0; matrix products, arithmetic and copies ran while one was open for 12% -> 0% of each run, Pallas kernels for 0% -> 0%
where the time goes in v1:
time: 28.4 us; the launch traced here: 28.3 us
  Pallas kernels  26.6 us (94%)
  local copies, waits for them, and re-layouts  1.62 us (6%)
    pallas_call x1, Pallas kernels, on_device(): pl.pallas_call(functools.partial(kernel, groups, pairs), out_shape=jax.Sh...  26.6 us
    unnamed x1, local copies, waits for them, and re-layouts  1.62 us

profile of v1, /device:TPU:0, one launch (start us, length us, event | category | flops | bytes accessed | tf_op | source)
XLA Modules:
  0.0 28.3 jit_solution(10484614266492227212)
XLA Ops:
  0.0 26.6 %shard_map.73 = bf16[3,128,256]{2,1,0:T(8,128)(2,1)} custom-call(bf16[3,128,256]{2,1,0:T(8,128)(2,1)} %bitcast.9, bf16[128,6,16,256]{3,2,1,0:T(8,128)(2,1)} %newell.1, bf16[2,2,128,256]{3,2,1,0:T(8,128)(2,1)} %constant.10.clone.y_fwd, bf16[2,2,128,256]{3,2,1,0:T(8,128)(2,1)} %constant.11.clone.y_inv, bf16[256,256]{1,0:T(8,128)(2,1)} %constant.12.clone.z_fwd, ...), custom_call_target="tpu_custom_call" | custom-call | tf_op jit(solution)/shard_map/pallas_call | solution.py:412
  26.6 1.6 %copy.10 = bf16[128,3,1,256]{3,0,2,1:T(8,128)(2,1)} copy(bf16[128,3,1,256]{3,0,2,1:T(8,128)(2,1)} %bitcast.8) | data formatting | bytes 393216

commit v2 on v1

--- a/solution.py
+++ b/solution.py
@@ -65,7 +65,7 @@
     groups, pairs, magnet, newell, y_fwd, y_inv, z_fwd, z_inv, rev, out,
     mag, nwl, yf, yi, zf, zi, rv, halo, spec, send, recv, kern, source, back, fields, stack,
     lap, result, load_sem, nwl_sem, pair_sem, halo_sem, fwd_send, fwd_recv, bwd_send, bwd_recv,
-    rel_send, rel_recv, out_sem,
+    rel_send, rel_recv, out_sem, hand,
 ):
     g = lax.axis_index("gx")
     c = lax.axis_index("yz")
@@ -75,12 +75,19 @@
     cells = groups
     half = magnet.shape[2] // 2
 
+    plane = math.gcd(groups, 4)
+    layers = groups // plane
+
+    def target(k):
+        layer, place = k // plane, lax.rem(k, plane)
+        layer = jnp.where(2 * (g // plane) < layers, layers - 1 - layer, layer)
+        return layer * plane + lax.rem(g + place, plane)
+
     barrier = pltpu.get_barrier_semaphore()
-    for r in range(1, groups):
-        pl.semaphore_signal(
-            barrier, inc=1, device_id=(lax.rem(g + r, groups), c), device_id_type=MESH
-        )
-    pl.semaphore_signal(barrier, inc=1, device_id=(g, other), device_id_type=MESH)
+
+    @pl.when(c == 0)
+    def _():
+        pl.semaphore_signal(barrier, inc=1, device_id=(g, 1), device_id_type=MESH)
 
     loads = []
     for comp in range(3):
@@ -108,7 +115,18 @@
     for copy in near:
         copy.start()
 
-    pl.semaphore_wait(barrier, groups)
+    @pl.when(c == 1)
+    def _():
+        pl.semaphore_wait(barrier, 1)
+        pl.semaphore_signal(hand.at[0], inc=1, device_id=(g, 0), device_id_type=MESH)
+
+    @pl.when(c == 0)
+    def _():
+        pl.semaphore_wait(hand.at[0], 1)
+        for r in range(1, groups):
+            pl.semaphore_signal(
+                barrier, inc=1, device_id=(lax.rem(g + r, groups), 0), device_id_type=MESH
+            )
 
     for comp in range(3):
         loads[comp].wait()
@@ -154,21 +172,42 @@
     for i in range(groups):
         send[i] = spec[pl.ds(i * own, own), :].astype(BF16)
 
-    forward = []
-    for r in range(1, groups):
-        to = lax.rem(g + r, groups)
-        forward.append(
-            pltpu.make_async_remote_copy(
-                src_ref=send.at[to],
-                dst_ref=recv.at[g],
-                send_sem=fwd_send.at[r],
-                recv_sem=fwd_recv.at[r],
-                device_id=(to, c),
-                device_id_type=MESH,
-            )
-        )
-    for copy in forward:
-        copy.start()
+    @pl.when(c == 0)
+    def _():
+        pl.semaphore_wait(barrier, groups - 1)
+        pl.semaphore_signal(hand.at[1], inc=1, device_id=(g, 1), device_id_type=MESH)
+
+    @pl.when(c == 1)
+    def _():
+        pl.semaphore_wait(hand.at[1], 1)
+
+    def forward(i):
+        r = lax.rem(i - g + groups, groups)
+        return pltpu.make_async_remote_copy(
+            src_ref=send.at[i],
+            dst_ref=recv.at[g],
+            send_sem=fwd_send.at[r],
+            recv_sem=fwd_recv.at[r],
+            device_id=(i, c),
+            device_id_type=MESH,
+        )
+
+    def arrival(buffer, sems, who):
+        r = lax.rem(g - who + groups, groups)
+        return pltpu.make_async_remote_copy(
+            src_ref=buffer.at[who],
+            dst_ref=buffer.at[who],
+            send_sem=fwd_send.at[r],
+            recv_sem=sems.at[r],
+            device_id=(who, c),
+            device_id_type=MESH,
+        )
+
+    for k in range(groups):
+        @pl.when(target(k) != g)
+        def _():
+            forward(target(k)).start()
+
     recv[g] = send[g]
 
     up = pltpu.make_async_remote_copy(
@@ -264,16 +303,32 @@
             source[j, 2 * comp] = new_re
             source[j, 2 * comp + 1] = new_im
 
-    unpack(g)
-    for r in range(1, groups):
-        forward[r - 1].wait_recv()
-        unpack(lax.rem(g + groups - r, groups))
+    for k in range(groups - 1, -1, -1):
+        who = target(k)
+
+        @pl.when(who != g)
+        def _():
+            arrival(recv, fwd_recv, who).wait_recv()
+
+        unpack(who)
 
     def k_of(entry, d):
         start = pl.multiple_of((entry * cells + d) * own, own)
         return kern[pl.ds(start, own), :]
 
-    def couple(i, carry):
+    def backward(i):
+        r = lax.rem(i - g + groups, groups)
+        return pltpu.make_async_remote_copy(
+            src_ref=back.at[i],
+            dst_ref=fields.at[c, g],
+            send_sem=bwd_send.at[r],
+            recv_sem=bwd_recv.at[r],
+            device_id=(i, c),
+            device_id_type=MESH,
+        )
+
+    def couple(k, carry):
+        i = target(k)
         acc = [jnp.zeros((own, half), F32) for _ in range(6)]
         for j in range(cells):
             d = jnp.abs(i - j)
@@ -295,40 +350,31 @@
             new_im = jnp.where(at_first, im + re_f, jnp.where(at_mirror, re - im_f, im))
             back[i, :, pl.ds(2 * comp * half, half)] = new_re.astype(BF16)
             back[i, :, pl.ds((2 * comp + 1) * half, half)] = new_im.astype(BF16)
+        before = target(jnp.maximum(k - 1, 0))
+
+        @pl.when(jnp.logical_and(k > 0, before != g))
+        def _():
+            backward(before).start()
+
         return carry
 
     lax.fori_loop(0, cells, couple, 0)
 
-    backward = []
-    for r in range(1, groups):
-        to = lax.rem(g + r, groups)
-        backward.append(
-            pltpu.make_async_remote_copy(
-                src_ref=back.at[to],
-                dst_ref=fields.at[c, g],
-                send_sem=bwd_send.at[r],
-                recv_sem=bwd_recv.at[r],
-                device_id=(to, c),
-                device_id_type=MESH,
-            )
-        )
-    for copy in backward:
-        copy.start()
+    @pl.when(target(groups - 1) != g)
+    def _():
+        backward(target(groups - 1)).start()
+
     fields[c, g] = back[g]
 
-    def relay(r):
-        who = lax.rem(g + groups - r, groups)
+    def relay(who):
         return pltpu.make_async_remote_copy(
             src_ref=fields.at[c, who],
             dst_ref=fields.at[c, who],
-            send_sem=rel_send.at[r],
-            recv_sem=rel_recv.at[r],
+            send_sem=rel_send.at[who],
+            recv_sem=rel_recv.at[who],
             device_id=(g, other),
             device_id_type=MESH,
         )
-
-    relays = [relay(r) for r in range(groups)]
-    relays[0].start()
 
     @pl.when(g == 0)
     def _():
@@ -351,11 +397,16 @@
         x_part = halo[0, comp].astype(F32) + halo[1, comp].astype(F32) - 2.0 * centre
         lap[comp] = EXCHANGE * (lap[comp] + x_part)
 
-    for r in range(1, groups):
-        backward[r - 1].wait_recv()
-        relays[r].start()
-    for r in range(groups):
-        relays[r].wait_recv()
+    for k in range(groups - 1, -1, -1):
+        who = target(k)
+
+        @pl.when(who != g)
+        def _():
+            arrival(fields.at[c], bwd_recv, who).wait_recv()
+
+        relay(who).start()
+    for i in range(groups):
+        relay(i).wait_recv()
     for part in range(2):
         for i in range(groups):
             stack[pl.ds((part * groups + i) * own, own), :] = fields[part, i].astype(F32)
@@ -381,8 +432,15 @@
         write.start()
         writes.append(write)
 
-    for copy in swap + far + forward + backward + relays:
+    for copy in swap + far:
         copy.wait_send()
+    for i in range(groups):
+        relay(i).wait_send()
+
+        @pl.when(i != g)
+        def _():
+            forward(i).wait_send()
+            backward(i).wait_send()
 
     @pl.when(g < groups - 1)
     def _():
@@ -444,6 +502,7 @@
             dma((groups,)),
             dma((groups,)),
             dma((3,)),
+            pltpu.SemaphoreType.REGULAR((2,)),
         ],
         compiler_params=pltpu.CompilerParams(collective_id=0, has_side_effects=True),
     )(planes, newell, *consts)

time: 28.4 us -> 27.2 us (0.958); the launches traced: 28.3 us -> 26.7 us
  Pallas kernels: 26.6 us -> 25.1 us
    pallas_call x1, Pallas kernels: 26.6 us -> 25.1 us  [on_device(): pl.pallas_call(functools.partial(kernel, groups, pairs), out_shape=jax.Sh...]
where the time goes in v2:
time: 27.2 us; the launch traced here: 26.7 us
  Pallas kernels  25.1 us (92%)
  local copies, waits for them, and re-layouts  1.62 us (6%)
    pallas_call x1, Pallas kernels, on_device(): pl.pallas_call(functools.partial(kernel, groups, pairs), out_shape=jax.Sh...  25.1 us
    unnamed x1, local copies, waits for them, and re-layouts  1.62 us

profile of v2, /device:TPU:0, one launch (start us, length us, event | category | flops | bytes accessed | tf_op | source)
XLA Modules:
  0.0 26.7 jit_solution(1273634563690825243)
XLA Ops:
  0.0 25.1 %shard_map.73 = bf16[3,128,256]{2,1,0:T(8,128)(2,1)} custom-call(bf16[3,128,256]{2,1,0:T(8,128)(2,1)} %bitcast.9, bf16[128,6,16,256]{3,2,1,0:T(8,128)(2,1)} %newell.1, bf16[2,2,128,256]{3,2,1,0:T(8,128)(2,1)} %constant.10.clone.y_fwd, bf16[2,2,128,256]{3,2,1,0:T(8,128)(2,1)} %constant.11.clone.y_inv, bf16[256,256]{1,0:T(8,128)(2,1)} %constant.12.clone.z_fwd, ...), custom_call_target="tpu_custom_call" | custom-call | tf_op jit(solution)/shard_map/pallas_call | solution.py:470
  25.1 1.6 %copy.10 = bf16[128,3,1,256]{3,0,2,1:T(8,128)(2,1)} copy(bf16[128,3,1,256]{3,0,2,1:T(8,128)(2,1)} %bitcast.8) | data formatting | bytes 393216

commit v3 on v2

--- a/solution.py
+++ b/solution.py
@@ -64,8 +64,8 @@
 def kernel(
     groups, pairs, magnet, newell, y_fwd, y_inv, z_fwd, z_inv, rev, out,
     mag, nwl, yf, yi, zf, zi, rv, halo, spec, send, recv, kern, source, back, fields, stack,
-    lap, result, load_sem, nwl_sem, pair_sem, halo_sem, fwd_send, fwd_recv, bwd_send, bwd_recv,
-    rel_send, rel_recv, out_sem, hand,
+    lap, load_sem, nwl_sem, pair_sem, halo_sem, fwd_send, fwd_recv, bwd_send, bwd_recv,
+    rel_send, rel_recv, hand,
 ):
     g = lax.axis_index("gx")
     c = lax.axis_index("yz")
@@ -210,30 +210,31 @@
 
     recv[g] = send[g]
 
-    up = pltpu.make_async_remote_copy(
-        src_ref=mag.at[:, pl.ds(0, rows), :],
-        dst_ref=halo.at[0],
-        send_sem=halo_sem.at[0],
-        recv_sem=halo_sem.at[1],
-        device_id=(lax.rem(g + 1, groups), c),
-        device_id_type=MESH,
-    )
-    down = pltpu.make_async_remote_copy(
-        src_ref=mag.at[:, pl.ds(0, rows), :],
-        dst_ref=halo.at[1],
-        send_sem=halo_sem.at[2],
-        recv_sem=halo_sem.at[3],
-        device_id=(lax.rem(g + groups - 1, groups), c),
-        device_id_type=MESH,
-    )
-
-    @pl.when(g < groups - 1)
-    def _():
-        up.start()
-
-    @pl.when(g > 0)
-    def _():
-        down.start()
+    def halo_copy(side, comp):
+        to = lax.rem(g + (1, groups - 1)[side], groups)
+        return pltpu.make_async_remote_copy(
+            src_ref=mag.at[comp, pl.ds(0, rows), :],
+            dst_ref=halo.at[side, comp],
+            send_sem=halo_sem.at[0, side, comp],
+            recv_sem=halo_sem.at[1, side, comp],
+            device_id=(to, c),
+            device_id_type=MESH,
+        )
+
+    has_next, has_last = g < groups - 1, g > 0
+
+    def halo_start(comps):
+        @pl.when(has_next)
+        def _():
+            for comp in comps:
+                halo_copy(0, comp).start()
+
+        @pl.when(has_last)
+        def _():
+            for comp in comps:
+                halo_copy(1, comp).start()
+
+    halo_start((0, 1))
 
     for copy in near:
         copy.wait()
@@ -364,6 +365,7 @@
     def _():
         backward(target(groups - 1)).start()
 
+    halo_start((2,))
     fields[c, g] = back[g]
 
     def relay(who):
@@ -376,35 +378,29 @@
             device_id_type=MESH,
         )
 
-    @pl.when(g == 0)
-    def _():
-        halo[0] = mag[:, pl.ds(0, rows), :]
-
-    @pl.when(g > 0)
-    def _():
-        up.wait_recv()
-
-    @pl.when(g == groups - 1)
-    def _():
-        halo[1] = mag[:, pl.ds(0, rows), :]
-
-    @pl.when(g < groups - 1)
-    def _():
-        down.wait_recv()
+    for k in range(groups - 1, -1, -1):
+        who = target(k)
+
+        @pl.when(who != g)
+        def _():
+            arrival(fields.at[c], bwd_recv, who).wait_recv()
+
+        relay(who).start()
+    for side, inside in enumerate((has_last, has_next)):
+        @pl.when(inside)
+        def _():
+            for comp in range(3):
+                halo_copy(side, comp).wait_recv()
+
+        @pl.when(jnp.logical_not(inside))
+        def _():
+            halo[side] = mag[:, pl.ds(0, rows), :]
 
     for comp in range(3):
         centre = mag[comp, pl.ds(0, rows), :].astype(F32)
         x_part = halo[0, comp].astype(F32) + halo[1, comp].astype(F32) - 2.0 * centre
         lap[comp] = EXCHANGE * (lap[comp] + x_part)
 
-    for k in range(groups - 1, -1, -1):
-        who = target(k)
-
-        @pl.when(who != g)
-        def _():
-            arrival(fields.at[c], bwd_recv, who).wait_recv()
-
-        relay(who).start()
     for i in range(groups):
         relay(i).wait_recv()
     for part in range(2):
@@ -414,7 +410,6 @@
     loads[6].wait()
     loads[7].wait()
     scale = 1.0 / (2 * rows * 2 * half)
-    writes = []
     for comp in range(3):
         modes = stack[:, pl.ds(2 * comp * half, 2 * half)].astype(BF16)
         cos_part = jnp.dot(yi[0], modes, preferred_element_type=F32)
@@ -427,10 +422,7 @@
             axis=1,
         ).astype(BF16)
         demag = jnp.dot(g_rows, zi[...], preferred_element_type=F32) * scale
-        result[comp] = (demag + lap[comp]).astype(BF16)
-        write = pltpu.make_async_copy(result.at[comp], out.at[comp], out_sem.at[comp])
-        write.start()
-        writes.append(write)
+        out[comp] = (demag + lap[comp]).astype(BF16)
 
     for copy in swap + far:
         copy.wait_send()
@@ -442,16 +434,11 @@
             forward(i).wait_send()
             backward(i).wait_send()
 
-    @pl.when(g < groups - 1)
-    def _():
-        up.wait_send()
-
-    @pl.when(g > 0)
-    def _():
-        down.wait_send()
-
-    for write in writes:
-        write.wait()
+    for side, inside in enumerate((has_next, has_last)):
+        @pl.when(inside)
+        def _():
+            for comp in range(3):
+                halo_copy(side, comp).wait_send()
 
 
 def on_device(magnet, newell, *consts):
@@ -469,9 +456,9 @@
     planes = jnp.transpose(magnet[:, :, 0, :], (1, 0, 2))
     field = pl.pallas_call(
         functools.partial(kernel, groups, pairs),
-        out_shape=jax.ShapeDtypeStruct(planes.shape, BF16),
+        out_shape=pltpu.VMEM(planes.shape, BF16),
         in_specs=[any_ref] * 7,
-        out_specs=any_ref,
+        out_specs=pl.BlockSpec(memory_space=pltpu.VMEM),
         scratch_shapes=[
             pltpu.VMEM((3, y_total, z_total), BF16),
             pltpu.VMEM((2, pairs, 6, groups, z_total), BF16),
@@ -490,18 +477,16 @@
             pltpu.VMEM((2, groups, own, wide), BF16),
             pltpu.VMEM((y_total, wide), F32),
             pltpu.VMEM((3, rows, z_total), F32),
-            pltpu.VMEM((3, rows, z_total), BF16),
             dma((8,)),
             dma((pairs,)),
             dma((2, 3 + pairs)),
-            dma((4,)),
+            dma((2, 2, 3)),
             dma((groups,)),
             dma((groups,)),
             dma((groups,)),
             dma((groups,)),
             dma((groups,)),
             dma((groups,)),
-            dma((3,)),
             pltpu.SemaphoreType.REGULAR((2,)),
         ],
         compiler_params=pltpu.CompilerParams(collective_id=0, has_side_effects=True),

time: 27.2 us -> 24.9 us (0.915); the launches traced: 26.7 us -> 24.8 us
  Pallas kernels: 25.1 us -> 24.1 us
  local copies, waits for them, and re-layouts: 1.62 us -> 0.68 us
    pallas_call x1, Pallas kernels: 25.1 us -> 24.1 us  [on_device(): pl.pallas_call(functools.partial(kernel, groups, pairs), out_shape=pltpu....]
    unnamed x1, local copies, waits for them, and re-layouts: 1.62 us -> 0.68 us
where the time goes in v3:
time: 24.9 us; the launch traced here: 24.8 us
  Pallas kernels  24.1 us (97%)
  local copies, waits for them, and re-layouts  0.68 us (3%)
    pallas_call x1, Pallas kernels, on_device(): pl.pallas_call(functools.partial(kernel, groups, pairs), out_shape=pltpu....  24.1 us
    unnamed x1, local copies, waits for them, and re-layouts  0.68 us

profile of v3, /device:TPU:0, one launch (start us, length us, event | category | flops | bytes accessed | tf_op | source)
XLA Modules:
  0.0 24.8 jit_solution(5026587225977610998)
XLA Ops:
  0.0 24.1 %shard_map.73 = bf16[3,128,256]{2,1,0:T(8,128)(2,1)S(1)} custom-call(bf16[3,128,256]{2,1,0:T(8,128)(2,1)} %bitcast.9, bf16[128,6,16,256]{3,2,1,0:T(8,128)(2,1)} %newell.1, bf16[2,2,128,256]{3,2,1,0:T(8,128)(2,1)} %constant.10.clone.y_fwd, bf16[2,2,128,256]{3,2,1,0:T(8,128)(2,1)} %constant.11.clone.y_inv, bf16[256,256]{1,0:T(8,128)(2,1)} %constant.12.clone.z_fwd, ...), custom_call_target="tpu_custom_call" | custom-call | tf_op jit(solution)/shard_map/pallas_call | solution.py:457
  24.1 0.7 %copy.10 = bf16[128,3,1,256]{3,0,2,1:T(8,128)(2,1)} copy(bf16[128,3,1,256]{3,0,2,1:T(8,128)(2,1)S(1)} %bitcast.8) | data formatting | bytes 393216
